TPU v7x, 32 devices: a whole 2x2x4 slice. The times are simulated.
32 devices in a mesh: blk: 16 (over z, y, x), slab: 2 (over core).
Axes of the slice: x: 2, y: 2, z: 4, core: 2. Of those that a mesh axis runs over, the one named last changes fastest.
Arguments:
- sinogram: bfloat16 [32, 8, 2048], P('blk', 'slab'), parts along dimension 1, may hold values from -6 to 6
- jitter: bfloat16 [32], P('blk'), may hold values from -0.29882812 to 0.29882812
- shift: int32 [32], replicated, may hold values from -8 to 8
Outputs:
- image: float32 [32, 8, 2048], P('blk', 'slab'), parts along dimension 1
There are 2 independent parts, one for each index of `slab`. A program takes and returns all parts, laid end to end along the dimension named above; an argument that names none is the same for every part. Nothing has to cross between parts.
All inputs are finite; a program needn't handle non-finite values.
Results may differ from a plain program's by a relative error of at most 0.0055.
Values may be sent and summed in bfloat16 or wider, within the bound.
No kernel may reach another device: no remote copies, remote signals or barrier semaphores. Data moves between devices by JAX's collectives and lax.ppermute only.
A program may use at most 64 MiB of HBM per device.

v0:
```python
import math

import jax
import jax.numpy as jnp
from jax import lax
from jax.sharding import PartitionSpec as P

ROWS_DEV = 2


def padded(cells, sides, width):
    for axis, dim in sides:
        count = lax.axis_size(axis)
        head = lax.slice_in_dim(cells, 0, width, axis=dim)
        tail = lax.slice_in_dim(cells, cells.shape[dim] - width, cells.shape[dim], axis=dim)
        cells = jnp.concatenate(
            [
                lax.ppermute(tail, axis, [(i, (i + 1) % count) for i in range(count)]),
                cells,
                lax.ppermute(head, axis, [((i + 1) % count, i) for i in range(count)]),
            ],
            axis=dim,
        )
    return cells


def ramp_matrix(bins):
    offsets = (
        jnp.arange(bins, dtype=jnp.int32)[None, :] - jnp.arange(bins, dtype=jnp.int32)[:, None]
    )
    safe = jnp.where(offsets == 0, 1, offsets).astype(jnp.float32)
    odd_part = jnp.where(offsets % 2 != 0, -1.0 / (math.pi**2 * safe * safe), jnp.float32(0.0))
    kernel = jnp.where(offsets == 0, jnp.float32(0.25), odd_part)
    return kernel.astype(jnp.bfloat16)


def contribute(frow, theta, offset, row_count, nrows):
    slices, bins = frow.shape
    nblocks = bins // 128
    pad_tiles = bins // 512 + 2
    tile_count = nblocks + 2 * pad_tiles
    pad_bins = pad_tiles * 128
    tiled = jnp.pad(frow, ((0, 0), (pad_bins, pad_bins))).reshape(slices, tile_count, 128)
    coords_x = (jnp.arange(bins, dtype=jnp.float32) - (bins - 1) / 2).reshape(nblocks, 128)
    row_pos = jnp.arange(row_count, dtype=jnp.int32).astype(jnp.float32) - (nrows - 1) / 2
    cosine = jnp.cos(theta)
    sine_part = jnp.sin(theta)
    center_bin = (bins - 1) / 2 + offset.astype(jnp.float32)
    coords = coords_x[None, :, :] * cosine + row_pos[:, None, None] * sine_part + center_bin
    lowest = jnp.minimum(coords[:, :, 0], coords[:, :, 127])
    first_tile = jnp.clip(
        (jnp.floor(lowest).astype(jnp.int32) + pad_bins) // 128, 0, tile_count - 3
    )
    first_tile = first_tile.reshape(row_count * nblocks)
    wanted = first_tile[:, None] + jnp.arange(3, dtype=jnp.int32)[None, :]
    selector = (
        wanted[:, :, None] == jnp.arange(tile_count, dtype=jnp.int32)[None, None, :]
    ).astype(jnp.bfloat16)
    strips = jnp.einsum(
        "njt,stk->nsjk", selector, tiled, preferred_element_type=jnp.float32
    ).astype(jnp.bfloat16)
    strips = strips.reshape(row_count * nblocks, slices, 3 * 128)
    detector = (
        first_tile[:, None] * 128 + jnp.arange(3 * 128, dtype=jnp.int32)[None, :] - pad_bins
    ).astype(jnp.float32)
    flat_coords = coords.reshape(row_count * nblocks, 128)
    weights = jnp.maximum(
        0.0, 1.0 - jnp.abs(detector[:, :, None] - flat_coords[:, None, :])
    ).astype(jnp.bfloat16)
    return jnp.einsum("nsb,nbc->nsc", strips, weights, preferred_element_type=jnp.float32)


def body(sinogram, jitter, shift):
    ang_dev, slices, bins = sinogram.shape
    width = lax.axis_size("blk")
    angles = width * ang_dev
    nrows = ROWS_DEV * width
    nblocks = bins // 128
    here = lax.axis_index("blk")
    extended = padded(jitter, (("blk", 0),), 1).astype(jnp.float32)
    weight = (1.0 + (extended[2:] - extended[:-2]) * 1.5) * (4.0 / math.sqrt(angles))
    ramp = ramp_matrix(bins)
    flat = jnp.dot(
        sinogram.reshape(ang_dev * slices, bins), ramp, preferred_element_type=jnp.float32
    )
    filtered = (flat.reshape(ang_dev, slices, bins) * weight[:, None, None]).astype(jnp.bfloat16)
    first = here * ang_dev
    count = ROWS_DEV * lax.axis_size("blk")

    def one_angle(position, accum):
        angle_id = first + position
        deviation = lax.dynamic_index_in_dim(jitter, position, 0, False).astype(jnp.float32)
        theta = (angle_id.astype(jnp.float32) + deviation) * math.pi / angles
        offset = lax.dynamic_index_in_dim(shift, angle_id, 0, False)
        frow = lax.dynamic_index_in_dim(filtered, position, 0, False)
        return accum + contribute(frow, theta, offset, count, nrows)

    accum = lax.fori_loop(
        0, ang_dev, one_angle, jnp.zeros((count * nblocks, slices, 128), jnp.float32)
    )
    return lax.psum_scatter(
        accum.reshape(count, nblocks, slices, 128)
        .transpose(0, 2, 1, 3)
        .reshape(count, slices, bins),
        "blk",
        scatter_dimension=0,
        tiled=True,
    )


def solution(mesh):
    in_specs = (P("blk", "slab", None), P("blk"), P())
    out_specs = P("blk", "slab", None)
    return jax.shard_map(body, mesh=mesh, in_specs=in_specs, out_specs=out_specs, check_vma=False)
```

profile of v0, /device:TPU:0, one launch (start us, length us, event | category | flops | bytes accessed | tf_op | source)
XLA Modules:
  0.0 243.2 jit_solution(2400293270538522140)
XLA Ops:
  6.5 1.3 fusion.38
  7.9 3.0 %collective-permute-start = (bf16[1]{0:T(256)(128)(2,1)}, bf16[1]{0:T(256)(128)(2,1)}, u32[]{:S(2)}, u32[]{:S(2)}) collective-permute-start(bf16[1]{0:T(256)(128)(2,1)} %get-tuple-element.201), channel_id=1, source_target_pairs={{0,2},{2,4},{4,6},{6,8},{8,10},{10,12},{12,14},{14,16},{16,18},{18... | collective-permute-start | bytes 14 | tf_op jit(solution)/shard_map/ppermute | solution.py:18
  10.8 4.0 %collective-permute-start.1 = (bf16[1]{0:T(256)(128)(2,1)}, bf16[1]{0:T(256)(128)(2,1)}, u32[]{:S(2)}, u32[]{:S(2)}) collective-permute-start(bf16[1]{0:T(256)(128)(2,1)} %get-tuple-element.202), channel_id=1, source_target_pairs={{2,0},{4,2},{6,4},{8,6},{10,8},{12,10},{14,12},{16,14},{18,16},{20... | collective-permute-start | bytes 14 | tf_op jit(solution)/shard_map/ppermute | solution.py:20
  14.8 0.8 reshape.204
  15.6 13.4 %fusion.27 = f32[8,2048]{1,0:T(8,128)S(1)} fusion(bf16[8,2048]{1,0:T(8,128)(2,1)S(1)} %reshape.204), kind=kOutput, calls=%fused_computation.49 | convolution fusion | flops 159383552 | bytes 98304 | tf_op jit(solution)/shard_map/dot_general | solution.py:83
  29.1 1.3 maximum_convert_fusion.4
  30.5 0.1 multiply_convert_fusion
  30.6 91.1 %while.16 = (s32[]{:T(128)}, f32[512,4,128]{2,1,0:T(4,128)}, bf16[2,4,2048]{2,1,0:T(4,128)(2,1)S(1)}, s32[]{:T(128)}, bf16[2]{0:T(256)(128)(2,1)S(1)}, /*index=5...) while((s32[]{:T(128)}, f32[512,4,128]{2,1,0:T(4,128)}, ...), condition=%wide.region_1.2_spmd.clone, body=%wide.region_0.1_spmd.clone.sunk | while | flops 373422176 | bytes 10977945 | solution.py:98
  30.6 0.6 dynamic_slice.41
  31.9 0.7 dynamic_slice.42
  33.3 0.1 add_add_fusion.2
  33.5 0.7 fusion.51
  34.4 0.6 convolution_convert_fusion.2
  35.0 1.4 copy.17
  36.4 0.1 add_convert_fusion.2
  36.6 0.1 add.470
  36.7 0.1 fusion.52
  36.9 39.0 %fusion.53 = f32[512,4,128]{2,1,0:T(4,128)} fusion(bf16[512,4,384]{2,1,0:T(4,128)(2,1)S(1)} %copy.17, f32[512,128]{1,0:T(8,128)S(1)} %fusion.52, f32[512,384]{1,0:T(8,128)S(1)} %add_convert_fusion.2, f32[512,4,128]{2,1,0:T(4,128)} %get-tuple-element.257, pred[]{:T(512)S(6)} %compare.34), kind=kOutput, calls=%fused_computation.3.clone.2 | convolution fusion | flops 327680000 | bytes 4718593 | tf_op jit(solution)/shard_map/while/body/eval_jaxpr/nsb,nbc->nsc/dot_general | solution.py:70
  75.9 0.6 dynamic_slice.41
  77.1 0.7 dynamic_slice.42
  78.6 0.1 add_add_fusion.2
  78.7 0.7 fusion.51
  79.6 0.6 convolution_convert_fusion.2
  80.2 1.4 copy.17
  81.7 0.1 add_convert_fusion.2
  82.0 0.1 fusion.52
  82.1 39.6 %fusion.53 = f32[512,4,128]{2,1,0:T(4,128)} fusion(bf16[512,4,384]{2,1,0:T(4,128)(2,1)S(1)} %copy.17, f32[512,128]{1,0:T(8,128)S(1)} %fusion.52, f32[512,384]{1,0:T(8,128)S(1)} %add_convert_fusion.2, f32[512,4,128]{2,1,0:T(4,128)} %get-tuple-element.257, pred[]{:T(512)S(6)} %compare.34), kind=kOutput, calls=%fused_computation.3.clone.2 | convolution fusion | flops 327680000 | bytes 4718593 | tf_op jit(solution)/shard_map/while/body/eval_jaxpr/nsb,nbc->nsc/dot_general | solution.py:70
  121.7 1.3 copy.15
  123.1 1.4 reshape.207
  124.5 0.6 dynamic-slice
  125.7 109.2 %all-reduce.4.cloned.1.call-done = f32[32,4,2048]{2,1,0:T(4,128)} async-done(((f32[32,4,2048]{2,1,0:T(4,128)}), f32[32,4,2048]{2,1,0:T(4,128)}) %all-reduce.4.cloned.1.call-update) | async-done | bytes 1048592
  234.8 1.5 constant_dynamic-slice_fusion
  (32 shorter events, 0.8 us)
Async XLA Ops:
  6.5 228.3 %all-reduce.4.cloned.1.call-start = ((), (), s32[]{:S(2)}) async-start(), calls=%async_computation | async-start | bytes 2097152
  7.9 21.2 %collective-permute-start = (bf16[1]{0:T(256)(128)(2,1)}, bf16[1]{0:T(256)(128)(2,1)}, u32[]{:S(2)}, u32[]{:S(2)}) collective-permute-start(bf16[1]{0:T(256)(128)(2,1)} %get-tuple-element.201), channel_id=1, source_target_pairs={{0,2},{2,4},{4,6},{6,8},{8,10},{10,12},{12,14},{14,16},{16,18},{18... | collective-permute-start | bytes 14 | tf_op jit(solution)/shard_map/ppermute | solution.py:18
  10.8 18.3 %collective-permute-start.1 = (bf16[1]{0:T(256)(128)(2,1)}, bf16[1]{0:T(256)(128)(2,1)}, u32[]{:S(2)}, u32[]{:S(2)}) collective-permute-start(bf16[1]{0:T(256)(128)(2,1)} %get-tuple-element.202), channel_id=1, source_target_pairs={{2,0},{4,2},{6,4},{8,6},{10,8},{12,10},{14,12},{16,14},{18,16},{20... | collective-permute-start | bytes 14 | tf_op jit(solution)/shard_map/ppermute | solution.py:20
  15.6 13.5 %copy-start = (bf16[2]{0:T(256)(128)(2,1)S(1)}, bf16[2]{0:T(256)(128)(2,1)}, u32[]{:S(2)}) copy-start(bf16[2]{0:T(256)(128)(2,1)} %param.6) | copy-start | bytes 16
  15.6 15.0 %copy-start.1 = (s32[32]{0:T(128)S(1)}, s32[32]{0:T(128)}, u32[]{:S(2)}) copy-start(s32[32]{0:T(128)} %param.7) | copy-start | bytes 388
  123.0 1.4 copy-start.2
Sparse Core Ops, SparseCore 0:
  124.6 110.2 all-reduce.3
where the time goes:
time: 244 us; the launch traced here: 243 us
  waiting for transfers between devices  109 us (45%)
  matrix products  93.2 us (38%)
  between operations  14.1 us (6%)
  local copies, waits for them, and re-layouts  12.9 us (5%)
  starting transfers between devices  6.97 us (3%)
  other arithmetic  3.74 us (2%)
  loops' own time  3.06 us (1%)
    unnamed x2, waiting for transfers between devices  109 us
    dot_general x2, matrix products, contribute(): jnp.einsum('nsb,nbc->nsc', strips, weights, preferred_element_type=jnp.fl...  78.6 us
    dot_general x1, matrix products, body(): jnp.dot(sinogram.reshape(ang_dev * slices, bins), ramp, preferred_element...  13.4 us
  transfers between devices with their start and end apart: 3, of which 1 were waited for; matrix products, arithmetic and copies ran while one was open for 6% of the time, Pallas kernels for 0%

commit v1 on v0

v1 whole, which is shorter than its diff:
```python
import functools
import math

import jax
import jax.numpy as jnp
from jax import lax
from jax.experimental import pallas as pl
from jax.experimental.pallas import tpu as pltpu
from jax.sharding import PartitionSpec as P

ROWS_DEV = 2
LANES = 128


def filter_kernel(sino_ref, jitter_ref, out_ref, ramp_ref):
    ang_dev, slices, bins = sino_ref.shape
    tiles = bins // LANES
    rows = ang_dev * slices
    lane = lax.broadcasted_iota(jnp.int32, (LANES, LANES), 1)
    row = lax.broadcasted_iota(jnp.int32, (LANES, LANES), 0)
    diff = lane - row
    odd = (diff & 1) == 1
    for d in range(2 * tiles - 1):
        n = diff + (d - tiles + 1) * LANES
        if d == tiles - 1:
            safe = jnp.where(n == 0, 1, n).astype(jnp.float32)
        else:
            safe = n.astype(jnp.float32)
        block = jnp.where(odd, -1.0 / (math.pi**2 * safe * safe), 0.0)
        if d == tiles - 1:
            block = jnp.where(n == 0, 0.25, block)
        ramp_ref[:, d * LANES : (d + 1) * LANES] = block.astype(jnp.bfloat16)
    sino = jnp.concatenate([sino_ref[a].astype(jnp.float32) for a in range(ang_dev)], axis=0)
    stacked = jnp.concatenate(
        [sino[:, i * LANES : (i + 1) * LANES] for i in range(tiles)], axis=0
    ).astype(jnp.bfloat16)
    parts = jnp.dot(stacked, ramp_ref[...], preferred_element_type=jnp.float32)
    for j in range(tiles):
        total = None
        for i in range(tiles):
            d = j - i + tiles - 1
            part = parts[i * rows : (i + 1) * rows, d * LANES : (d + 1) * LANES]
            total = part if total is None else total + part
        out_ref[:, j * LANES : (j + 1) * LANES] = total.astype(jnp.bfloat16)
    sub = lax.broadcasted_iota(jnp.int32, (rows, LANES), 0)
    spread = jnp.zeros((rows, LANES), jnp.float32)
    for a in range(ang_dev):
        value = jitter_ref[:, a : a + 1].astype(jnp.float32)
        spread = jnp.where(sub // slices == a, jnp.broadcast_to(value, (rows, LANES)), spread)
    out_ref[:, bins:] = spread.astype(jnp.bfloat16)


def project_kernel(
    here_ref, shift_ref, gath_ref, out_ref, val_ref, dif_ref, jit_ref, cos_ref, off_ref,
    tile_vmem, tile_smem, sem, *, nrows, bins, slices
):
    width = gath_ref.shape[0]
    angles = 2 * width
    tiles = bins // LANES
    padded = tiles + 2
    here = here_ref[0]
    lane = lax.broadcasted_iota(jnp.int32, (8, LANES), 1)
    sub = lax.broadcasted_iota(jnp.int32, (8, LANES), 0)
    first_half = sub < slices
    last_lane = lane == LANES - 1
    lane_f = lane.astype(jnp.float32)
    half = (bins - 1) / 2
    row_first = (here * ROWS_DEV).astype(jnp.float32) - (nrows - 1) / 2
    row_pos = row_first + jnp.where(first_half, 0.0, 1.0)

    def both(x):
        other = pltpu.roll(x, slices, axis=0)
        return jnp.where(first_half, x, other), jnp.where(first_half, other, x)

    def spread_jitter(d, carry):
        one, two = both(gath_ref[d, :, bins:].astype(jnp.float32))
        jit_ref[2 * d] = one
        jit_ref[2 * d + 1] = two
        return carry

    lax.fori_loop(0, width, spread_jitter, 0)

    def prepare(d, carry):
        raw = gath_ref[d, :, bins:].astype(jnp.float32)
        position = (2 * d).astype(jnp.float32) + jnp.where(first_half, 0.0, 1.0)
        theta = (position + raw) * math.pi / angles
        cosines = both(jnp.cos(theta))
        sines = both(jnp.sin(theta))
        scales = []
        for p in range(2):
            a = 2 * d + p
            after = jit_ref[lax.rem(a + 1, angles)]
            before = jit_ref[lax.rem(a + angles - 1, angles)]
            scales.append((1.0 + (after - before) * 1.5) * (4.0 / math.sqrt(angles)))
            c, s = cosines[p], sines[p]
            center = half + LANES + shift_ref[a].astype(jnp.float32)
            off = row_pos * s + center
            cos_ref[a] = c
            off_ref[a] = (lane_f - half) * c + off
            lowest = (lane_f * LANES - half + jnp.where(c < 0, LANES - 1.0, 0.0)) * c + off
            lowest = jnp.minimum(lowest, pltpu.roll(lowest, slices, axis=0)) - 0.25
            first_tile = jnp.clip(lowest.astype(jnp.int32) >> 7, 0, padded - 2)
            tile_vmem[pl.ds(a, 1), :] = first_tile[0:1, :]
        zero = jnp.zeros((8, LANES), jnp.float32)
        current, moved = zero, zero
        for t in range(padded):
            if t + 1 < padded - 1:
                following = gath_ref[d, :, t * LANES : (t + 1) * LANES].astype(jnp.float32)
                following_moved = pltpu.roll(following, LANES - 1, axis=1)
            else:
                following, following_moved = zero, zero
            step = jnp.where(last_lane, following_moved, moved) - current
            values = both(current) if 0 < t < padded - 1 else (zero, zero)
            steps = both(step)
            for p in range(2):
                val_ref[(2 * d + p) * padded + t] = values[p] * scales[p]
                dif_ref[(2 * d + p) * padded + t] = steps[p] * scales[p]
            current, moved = following, following_moved
        return carry

    lax.fori_loop(0, width, prepare, 0)
    copy = pltpu.make_async_copy(tile_vmem, tile_smem, sem)
    copy.start()
    copy.wait()

    def one_angle(a, accum):
        c = cos_ref[a]
        start = off_ref[a]
        result = []
        for j in range(tiles):
            t = tile_smem[a, j]
            at = a * padded + t
            coord = start + c * float(j * LANES)
            lower = coord.astype(jnp.int32)
            frac = coord - lower.astype(jnp.float32)
            local = lower - t * LANES
            inner = local & (LANES - 1)
            near = local < LANES
            take = functools.partial(jnp.take_along_axis, axis=1, mode="promise_in_bounds")
            value = jnp.where(near, take(val_ref[at], inner), take(val_ref[at + 1], inner))
            step = jnp.where(near, take(dif_ref[at], inner), take(dif_ref[at + 1], inner))
            result.append(accum[j] + (value + frac * step))
        return tuple(result)

    init = tuple(jnp.zeros((8, LANES), jnp.float32) for _ in range(tiles))
    accum = lax.fori_loop(0, angles, one_angle, init)
    for j in range(tiles):
        for r in range(ROWS_DEV):
            out_ref[r, :, j * LANES : (j + 1) * LANES] = accum[j][r * slices : (r + 1) * slices]


def body(sinogram, jitter, shift):
    ang_dev, slices, bins = sinogram.shape
    width = lax.axis_size("blk")
    angles = width * ang_dev
    nrows = ROWS_DEV * width
    padded = bins // LANES + 2
    here = lax.axis_index("blk").astype(jnp.int32).reshape(1)
    payload = pl.pallas_call(
        filter_kernel,
        out_shape=jax.ShapeDtypeStruct((ang_dev * slices, bins + LANES), jnp.bfloat16),
        scratch_shapes=[pltpu.VMEM((LANES, (2 * (bins // LANES) - 1) * LANES), jnp.bfloat16)],
        name="filter",
    )(sinogram, jitter.reshape(1, ang_dev))
    gathered = lax.all_gather(payload, "blk", axis=0, tiled=False)
    return pl.pallas_call(
        functools.partial(project_kernel, nrows=nrows, bins=bins, slices=slices),
        in_specs=[
            pl.BlockSpec(memory_space=pltpu.SMEM),
            pl.BlockSpec(memory_space=pltpu.SMEM),
            pl.BlockSpec(memory_space=pltpu.VMEM),
        ],
        out_shape=jax.ShapeDtypeStruct((ROWS_DEV, slices, bins), jnp.float32),
        scratch_shapes=[
            pltpu.VMEM((angles * padded, 8, LANES), jnp.float32),
            pltpu.VMEM((angles * padded, 8, LANES), jnp.float32),
            pltpu.VMEM((angles, 8, LANES), jnp.float32),
            pltpu.VMEM((angles, 8, LANES), jnp.float32),
            pltpu.VMEM((angles, 8, LANES), jnp.float32),
            pltpu.VMEM((angles, LANES), jnp.int32),
            pltpu.SMEM((angles, LANES), jnp.int32),
            pltpu.SemaphoreType.DMA(()),
        ],
        name="project",
    )(here, shift, gathered)


def solution(mesh):
    in_specs = (P("blk", "slab", None), P("blk"), P())
    out_specs = P("blk", "slab", None)
    return jax.shard_map(body, mesh=mesh, in_specs=in_specs, out_specs=out_specs, check_vma=False)
```

time: 244 us -> 61.6 us (0.25)
  waiting for transfers between devices: 109 us -> 0 us
  matrix products: 93.2 us -> 0 us
  blocking collectives: 0 us -> 48.3 us
  between operations: 14.1 us -> 0.01 us
  Pallas kernels: 0 us -> 13.1 us
  local copies, waits for them, and re-layouts: 12.9 us -> 0 us
  starting transfers between devices: 6.97 us -> 0 us
  other arithmetic: 3.74 us -> 0 us
  loops' own time: 3.06 us -> 0 us
    unnamed x2 -> x0, waiting for transfers between devices: 109 us -> none
    dot_general x5 -> x0, matrix products: 93.2 us -> none  [the longest x2 78.6 us: contribute(): jnp.einsum('nsb,nbc->nsc', strips, weights, preferred_element_type=jnp.fl...]
    all_gather x0 -> x1, blocking collectives: none -> 48.3 us  [body(): gathered = lax.all_gather(payload, 'blk', axis=0, tiled=False)]
    pallas_call x0 -> x2, Pallas kernels: none -> 13.1 us  [the longest x1 10.8 us: body(): pl.pallas_call(functools.partial(project_kernel, nrows=nrows, bins=bins,...]
    ppermute x2 -> x0, starting transfers between devices: 6.96 us -> none  [the longest x1 4 us: padded(): lax.ppermute(head, axis, [((i + 1) % count, i) for i in range(count)])]
    reshape x8 -> x0, local copies, waits for them, and re-layouts: 6.45 us -> none  [the longest x2 2.89 us: contribute(): strips = strips.reshape(row_count * nblocks, slices, 3 * 128)]
    another operation x1 -> x0, loops' own time: 3.06 us -> none  [body(): lax.fori_loop(0, ang_dev, one_angle, jnp.zeros((count * nblocks, slices,...]
    dynamic_slice x4 -> x0, local copies, waits for them, and re-layouts: 2.52 us -> none  [the longest x2 1.3 us: one_angle(): lax.dynamic_index_in_dim(jitter, position, 0, False).astype(jnp.float32)]
  transfers between devices with their start and end apart: 3 -> 0, of which waited for: 1 -> 0; matrix products, arithmetic and copies ran while one was open for 6% -> 0% of each run, Pallas kernels for 0% -> 0%
where the time goes in v1:
time: 61.6 us; the launch traced here: 61.4 us
  blocking collectives  48.3 us (78%)
  Pallas kernels  13.1 us (21%)
    all_gather x1, blocking collectives, body(): gathered = lax.all_gather(payload, 'blk', axis=0, tiled=False)  48.3 us
    pallas_call x1, Pallas kernels, body(): pl.pallas_call(functools.partial(project_kernel, nrows=nrows, bins=bins,...  10.8 us
    pallas_call x1, Pallas kernels, body(): pl.pallas_call(filter_kernel, out_shape=jax.ShapeDtypeStruct((ang_dev * s...  2.34 us

profile of v1, /device:TPU:0, one launch (start us, length us, event | category | flops | bytes accessed | tf_op | source)
XLA Modules:
  0.0 61.4 jit_solution(9816905334788072607)
XLA Ops:
  0.0 2.3 %filter.1 = bf16[8,2176]{1,0:T(8,128)(2,1)} custom-call(bf16[2,4,2048]{2,1,0:T(4,128)(2,1)} %sino_ref.1, bf16[1,2]{1,0:T(2,128)(2,1)} %bitcast.4), custom_call_target="tpu_custom_call" | custom-call | tf_op jit(solution)/shard_map/filter/pallas_call | solution.py:159
  2.3 48.3 %all-gather = bf16[128,2176]{1,0:T(8,128)(2,1)} all-gather(bf16[8,2176]{1,0:T(8,128)(2,1)} %filter.1), channel_id=2, replica_groups=mesh['blk'=16,'slab'=2] {'blk'}, dimensions={0}, use_global_device_ids=true | all-gather | bytes 591872 | tf_op jit(solution)/shard_map/all_gather | solution.py:165
  50.6 10.8 %project.1 = f32[2,4,2048]{2,1,0:T(4,128)} custom-call(s32[1]{0:T(128)} %bitcast.here_ref, s32[32]{0:T(128)} %shift_ref.1, bf16[16,8,2176]{2,1,0:T(8,128)(2,1)} %bitcast.3), custom_call_target="tpu_custom_call" | custom-call | tf_op jit(solution)/shard_map/project/pallas_call | solution.py:166

commit v2 on v1

--- a/solution.py
+++ b/solution.py
@@ -50,11 +50,24 @@
     out_ref[:, bins:] = spread.astype(jnp.bfloat16)
 
 
-def project_kernel(
-    here_ref, shift_ref, gath_ref, out_ref, val_ref, dif_ref, jit_ref, cos_ref, off_ref,
-    tile_vmem, tile_smem, sem, *, nrows, bins, slices
-):
-    width = gath_ref.shape[0]
+def lane_take(x, index):
+    numbers = lax.GatherDimensionNumbers(
+        offset_dims=(),
+        collapsed_slice_dims=(1,),
+        start_index_map=(1,),
+        operand_batching_dims=(0,),
+        start_indices_batching_dims=(0,),
+    )
+    return lax.gather(
+        x, index[:, :, None], numbers, (1, 1), mode=lax.GatherScatterMode.PROMISE_IN_BOUNDS
+    )
+
+
+def project_kernel(here_ref, order_ref, shift_ref, *refs, pieces, nrows, bins, slices):
+    piece_refs, out_ref = refs[:pieces], refs[pieces]
+    val_ref, dif_ref, jit_ref, cos_ref, off_ref, low_ref = refs[pieces + 1 : pieces + 7]
+    tile_vmem, tile_smem, sem = refs[pieces + 7 :]
+    width = sum(ref.shape[0] for ref in piece_refs)
     angles = 2 * width
     tiles = bins // LANES
     padded = tiles + 2
@@ -72,16 +85,25 @@
         other = pltpu.roll(x, slices, axis=0)
         return jnp.where(first_half, x, other), jnp.where(first_half, other, x)
 
-    def spread_jitter(d, carry):
-        one, two = both(gath_ref[d, :, bins:].astype(jnp.float32))
+    def spread_jitter(i, carry, piece, at):
+        one, two = both(piece[i, :, bins:].astype(jnp.float32))
+        d = here ^ order_ref[at + i]
         jit_ref[2 * d] = one
         jit_ref[2 * d + 1] = two
         return carry
 
-    lax.fori_loop(0, width, spread_jitter, 0)
-
-    def prepare(d, carry):
-        raw = gath_ref[d, :, bins:].astype(jnp.float32)
+    def each_device(function):
+        at = 0
+        for piece in piece_refs:
+            count = piece.shape[0]
+            lax.fori_loop(0, count, functools.partial(function, piece=piece, at=at), 0)
+            at += count
+
+    each_device(spread_jitter)
+
+    def prepare(i, carry, piece, at):
+        d = here ^ order_ref[at + i]
+        raw = piece[i, :, bins:].astype(jnp.float32)
         position = (2 * d).astype(jnp.float32) + jnp.where(first_half, 0.0, 1.0)
         theta = (position + raw) * math.pi / angles
         cosines = both(jnp.cos(theta))
@@ -95,17 +117,19 @@
             c, s = cosines[p], sines[p]
             center = half + LANES + shift_ref[a].astype(jnp.float32)
             off = row_pos * s + center
+            low = (jnp.where(c < 0, LANES - 1.0, 0.0) - half) * c + off
             cos_ref[a] = c
             off_ref[a] = (lane_f - half) * c + off
-            lowest = (lane_f * LANES - half + jnp.where(c < 0, LANES - 1.0, 0.0)) * c + off
-            lowest = jnp.minimum(lowest, pltpu.roll(lowest, slices, axis=0)) - 0.25
+            low_ref[a] = low
+            lowest = low + c * (lane_f * LANES)
+            lowest = jnp.minimum(lowest, pltpu.roll(lowest, slices, axis=0))
             first_tile = jnp.clip(lowest.astype(jnp.int32) >> 7, 0, padded - 2)
             tile_vmem[pl.ds(a, 1), :] = first_tile[0:1, :]
         zero = jnp.zeros((8, LANES), jnp.float32)
         current, moved = zero, zero
         for t in range(padded):
             if t + 1 < padded - 1:
-                following = gath_ref[d, :, t * LANES : (t + 1) * LANES].astype(jnp.float32)
+                following = piece[i, :, t * LANES : (t + 1) * LANES].astype(jnp.float32)
                 following_moved = pltpu.roll(following, LANES - 1, axis=1)
             else:
                 following, following_moved = zero, zero
@@ -118,7 +142,7 @@
             current, moved = following, following_moved
         return carry
 
-    lax.fori_loop(0, width, prepare, 0)
+    each_device(prepare)
     copy = pltpu.make_async_copy(tile_vmem, tile_smem, sem)
     copy.start()
     copy.wait()
@@ -126,19 +150,20 @@
     def one_angle(a, accum):
         c = cos_ref[a]
         start = off_ref[a]
+        low = low_ref[a]
         result = []
         for j in range(tiles):
             t = tile_smem[a, j]
             at = a * padded + t
-            coord = start + c * float(j * LANES)
-            lower = coord.astype(jnp.int32)
+            along = c * float(j * LANES)
+            coord = start + along
+            bottom = (low + along).astype(jnp.int32)
+            lower = jnp.minimum(coord.astype(jnp.int32), bottom + (LANES - 1))
             frac = coord - lower.astype(jnp.float32)
-            local = lower - t * LANES
-            inner = local & (LANES - 1)
-            near = local < LANES
-            take = functools.partial(jnp.take_along_axis, axis=1, mode="promise_in_bounds")
-            value = jnp.where(near, take(val_ref[at], inner), take(val_ref[at + 1], inner))
-            step = jnp.where(near, take(dif_ref[at], inner), take(dif_ref[at + 1], inner))
+            near = lane >= bottom - t * LANES
+            inner = lower & (LANES - 1)
+            value = lane_take(jnp.where(near, val_ref[at], val_ref[at + 1]), inner)
+            step = lane_take(jnp.where(near, dif_ref[at], dif_ref[at + 1]), inner)
             result.append(accum[j] + (value + frac * step))
         return tuple(result)
 
@@ -147,6 +172,13 @@
     for j in range(tiles):
         for r in range(ROWS_DEV):
             out_ref[r, :, j * LANES : (j + 1) * LANES] = accum[j][r * slices : (r + 1) * slices]
+
+
+def exchange(pieces, width, stride, group):
+    return [
+        lax.ppermute(pieces, "blk", [(i, i ^ (k * stride)) for i in range(width)])
+        for k in range(1, group)
+    ]
 
 
 def body(sinogram, jitter, shift):
@@ -162,18 +194,31 @@
         scratch_shapes=[pltpu.VMEM((LANES, (2 * (bins // LANES) - 1) * LANES), jnp.bfloat16)],
         name="filter",
     )(sinogram, jitter.reshape(1, ang_dev))
-    gathered = lax.all_gather(payload, "blk", axis=0, tiled=False)
+    assert width & (width - 1) == 0
+    group_bits = width.bit_length() - 1
+    pieces = [payload[None]]
+    order = [0]
+    while group_bits:
+        group = 4 if group_bits >= 2 else 2
+        group_bits -= group.bit_length() - 1
+        stride = 1 << group_bits
+        held = pieces[0] if len(pieces) == 1 else jnp.concatenate(pieces, axis=0)
+        order = [o ^ (k * stride) for k in range(group) for o in order]
+        pieces = [held] + exchange(held, width, stride, group)
+    order = jnp.asarray(order, jnp.int32)
     return pl.pallas_call(
-        functools.partial(project_kernel, nrows=nrows, bins=bins, slices=slices),
+        functools.partial(project_kernel, pieces=len(pieces), nrows=nrows, bins=bins, slices=slices),
         in_specs=[
             pl.BlockSpec(memory_space=pltpu.SMEM),
             pl.BlockSpec(memory_space=pltpu.SMEM),
-            pl.BlockSpec(memory_space=pltpu.VMEM),
-        ],
+            pl.BlockSpec(memory_space=pltpu.SMEM),
+        ]
+        + [pl.BlockSpec(memory_space=pltpu.VMEM)] * len(pieces),
         out_shape=jax.ShapeDtypeStruct((ROWS_DEV, slices, bins), jnp.float32),
         scratch_shapes=[
             pltpu.VMEM((angles * padded, 8, LANES), jnp.float32),
             pltpu.VMEM((angles * padded, 8, LANES), jnp.float32),
+            pltpu.VMEM((angles, 8, LANES), jnp.float32),
             pltpu.VMEM((angles, 8, LANES), jnp.float32),
             pltpu.VMEM((angles, 8, LANES), jnp.float32),
             pltpu.VMEM((angles, 8, LANES), jnp.float32),
@@ -182,7 +227,7 @@
             pltpu.SemaphoreType.DMA(()),
         ],
         name="project",
-    )(here, shift, gathered)
+    )(here, order, shift, *pieces)
 
 
 def solution(mesh):

time: 61.6 us -> 31.7 us (0.51)
  blocking collectives: 48.3 us -> 0 us
  waiting for transfers between devices: 0 us -> 9.21 us
  starting transfers between devices: 0 us -> 9.2 us
  Pallas kernels: 13.1 us -> 11.5 us
  other arithmetic: 0 us -> 0.79 us
  local copies, waits for them, and re-layouts: 0 us -> 0.71 us
    all_gather x1 -> x0, blocking collectives: 48.3 us -> none  [body(): gathered = lax.all_gather(payload, 'blk', axis=0, tiled=False)]
    ppermute x0 -> x6, waiting for transfers between devices: none -> 9.21 us  [exchange(): lax.ppermute(pieces, 'blk', [(i, i ^ k * stride) for i in range(width)])]
    ppermute x0 -> x6, starting transfers between devices: none -> 9.2 us  [exchange(): lax.ppermute(pieces, 'blk', [(i, i ^ k * stride) for i in range(width)])]
    pallas_call x1, Pallas kernels: 10.8 us -> 9.15 us  [body(): pl.pallas_call(functools.partial(project_kernel, pieces=len(pieces), nrow...]
    concatenate x0 -> x1, other arithmetic: none -> 0.79 us  [body(): held = pieces[0] if len(pieces) == 1 else jnp.concatenate(pieces, axis=0)]
    unnamed x0 -> x8, local copies, waits for them, and re-layouts: none -> 0.71 us
  transfers between devices with their start and end apart: 0 -> 6, of which waited for: 0 -> 4; matrix products, arithmetic and copies ran while one was open for 0% -> 0% of each run, Pallas kernels for 0% -> 0%
where the time goes in v2:
time: 31.7 us; the launch traced here: 31.4 us
  Pallas kernels  11.5 us (36%)
  waiting for transfers between devices  9.21 us (29%)
  starting transfers between devices  9.2 us (29%)
  other arithmetic  0.79 us (2%)
  local copies, waits for them, and re-layouts  0.71 us (2%)
    ppermute x6, waiting for transfers between devices, exchange(): lax.ppermute(pieces, 'blk', [(i, i ^ k * stride) for i in range(width)])  9.21 us
    ppermute x6, starting transfers between devices, exchange(): lax.ppermute(pieces, 'blk', [(i, i ^ k * stride) for i in range(width)])  9.2 us
    pallas_call x1, Pallas kernels, body(): pl.pallas_call(functools.partial(project_kernel, pieces=len(pieces), nrow...  9.15 us
    pallas_call x1, Pallas kernels, body(): pl.pallas_call(filter_kernel, out_shape=jax.ShapeDtypeStruct((ang_dev * s...  2.34 us
    concatenate x1, other arithmetic, body(): held = pieces[0] if len(pieces) == 1 else jnp.concatenate(pieces, axis=0)  0.79 us
    unnamed x8, local copies, waits for them, and re-layouts  0.71 us
  transfers between devices with their start and end apart: 6, of which 4 were waited for; matrix products, arithmetic and copies ran while one was open for 0% of the time, Pallas kernels for 0%

profile of v2, /device:TPU:0, one launch (start us, length us, event | category | flops | bytes accessed | tf_op | source)
XLA Modules:
  0.0 31.4 jit_solution(8374391353083192447)
XLA Ops:
  0.0 2.3 %filter.1 = bf16[8,2176]{1,0:T(8,128)(2,1)} custom-call(bf16[2,4,2048]{2,1,0:T(4,128)(2,1)} %sino_ref.1, bf16[1,2]{1,0:T(2,128)(2,1)} %bitcast.7), custom_call_target="tpu_custom_call" | custom-call | tf_op jit(solution)/shard_map/filter/pallas_call | solution.py:191
  2.3 5.1 %collective-permute-start.2 = (bf16[1,8,2176]{2,1,0:T(8,128)(2,1)}, bf16[1,8,2176]{2,1,0:T(8,128)(2,1)S(1)}, u32[]{:S(2)}, u32[]{:S(2)}) collective-permute-start(bf16[1,8,2176]{2,1,0:T(8,128)(2,1)} %bitcast.3), channel_id=1, source_target_pairs={{0,24},{2,26},{4,28},{6,30},{8,16},{10,18},{12,20},{14,22},{16,8},... | collective-permute-start | bytes 104456 | tf_op jit(solution)/shard_map/ppermute | solution.py:179
  7.4 0.0 collective-permute-start.1
  7.4 0.6 %collective-permute-start = (bf16[1,8,2176]{2,1,0:T(8,128)(2,1)}, bf16[1,8,2176]{2,1,0:T(8,128)(2,1)S(1)}, u32[]{:S(2)}, u32[]{:S(2)}) collective-permute-start(bf16[1,8,2176]{2,1,0:T(8,128)(2,1)} %bitcast.5), channel_id=1, source_target_pairs={{0,8},{2,10},{4,12},{6,14},{8,0},{10,2},{12,4},{14,6},{16,24},{18,... | collective-permute-start | bytes 104456 | tf_op jit(solution)/shard_map/ppermute | solution.py:179
  8.0 1.6 %collective-permute-done.2 = bf16[1,8,2176]{2,1,0:T(8,128)(2,1)S(1)} collective-permute-done((bf16[1,8,2176]{2,1,0:T(8,128)(2,1)}, bf16[1,8,2176]{2,1,0:T(8,128)(2,1)S(1)}, u32[]{:S(2)}, u32[]{:S(2)}) %collective-permute-start.2) | collective-permute-done | bytes 34848 | tf_op jit(solution)/shard_map/ppermute | solution.py:179
  9.5 2.9 %collective-permute-done.1 = bf16[1,8,2176]{2,1,0:T(8,128)(2,1)S(1)} collective-permute-done((bf16[1,8,2176]{2,1,0:T(8,128)(2,1)}, bf16[1,8,2176]{2,1,0:T(8,128)(2,1)S(1)}, u32[]{:S(2)}, u32[]{:S(2)}) %collective-permute-start.1) | collective-permute-done | bytes 34848 | tf_op jit(solution)/shard_map/ppermute | solution.py:179
  12.5 0.0 collective-permute-done
  12.5 0.8 %pad_maximum_fusion.refs_0_ = bf16[4,8,2176]{2,1,0:T(8,128)(2,1)S(1)} fusion(bf16[1,8,2176]{2,1,0:T(8,128)(2,1)S(1)} %collective-permute-done.2, bf16[1,8,2176]{2,1,0:T(8,128)(2,1)S(1)} %collective-permute-done.1, bf16[1,8,2176]{2,1,0:T(8,128)(2,1)S(1)} %collective-permute-done, bf16[1,8,2176]{2,1,0:T(8,128)(2,1)} %bitcast.6), kind=kLoop, calls=%fused_computation | loop fusion | flops 208896 | bytes 278528 | tf_op jit(solution)/shard_map/concatenate | solution.py:205
  13.3 0.0 copy-start
  13.3 2.5 %collective-permute-start.5 = (bf16[4,8,2176]{2,1,0:T(8,128)(2,1)S(1)}, bf16[4,8,2176]{2,1,0:T(8,128)(2,1)S(1)}, u32[]{:S(2)}, u32[]{:S(2)}) collective-permute-start(bf16[4,8,2176]{2,1,0:T(8,128)(2,1)S(1)} %pad_maximum_fusion.refs_0_), channel_id=1, source_target_pairs={{0,6},{2,4},{4,2},{6,0},{8,14},{10,12},{12,10},{14,8},{16,22},{18,... | collective-permute-start | bytes 417800 | tf_op jit(solution)/shard_map/ppermute | solution.py:179
  15.8 0.5 %collective-permute-start.4 = (bf16[4,8,2176]{2,1,0:T(8,128)(2,1)S(1)}, bf16[4,8,2176]{2,1,0:T(8,128)(2,1)S(1)}, u32[]{:S(2)}, u32[]{:S(2)}) collective-permute-start(bf16[4,8,2176]{2,1,0:T(8,128)(2,1)S(1)} %pad_maximum_fusion.refs_0_), channel_id=1, source_target_pairs={{0,4},{2,6},{4,0},{6,2},{8,12},{10,14},{12,8},{14,10},{16,20},{18,... | collective-permute-start | bytes 417800 | tf_op jit(solution)/shard_map/ppermute | solution.py:179
  16.3 0.5 %collective-permute-start.3 = (bf16[4,8,2176]{2,1,0:T(8,128)(2,1)S(1)}, bf16[4,8,2176]{2,1,0:T(8,128)(2,1)S(1)}, u32[]{:S(2)}, u32[]{:S(2)}) collective-permute-start(bf16[4,8,2176]{2,1,0:T(8,128)(2,1)S(1)} %pad_maximum_fusion.refs_0_), channel_id=1, source_target_pairs={{0,2},{2,0},{4,6},{6,4},{8,10},{10,8},{12,14},{14,12},{16,18},{18,... | collective-permute-start | bytes 417800 | tf_op jit(solution)/shard_map/ppermute | solution.py:179
  16.8 3.9 %collective-permute-done.5.refs_3_ = bf16[4,8,2176]{2,1,0:T(8,128)(2,1)S(1)} collective-permute-done((bf16[4,8,2176]{2,1,0:T(8,128)(2,1)S(1)}, bf16[4,8,2176]{2,1,0:T(8,128)(2,1)S(1)}, u32[]{:S(2)}, u32[]{:S(2)}) %collective-permute-start.5) | collective-permute-done | bytes 139296 | tf_op jit(solution)/shard_map/ppermute | solution.py:179
  20.8 0.0 copy-start.1
  20.8 0.8 %collective-permute-done.4.refs_2_ = bf16[4,8,2176]{2,1,0:T(8,128)(2,1)S(1)} collective-permute-done((bf16[4,8,2176]{2,1,0:T(8,128)(2,1)S(1)}, bf16[4,8,2176]{2,1,0:T(8,128)(2,1)S(1)}, u32[]{:S(2)}, u32[]{:S(2)}) %collective-permute-start.4) | collective-permute-done | bytes 139296 | tf_op jit(solution)/shard_map/ppermute | solution.py:179
  21.6 0.0 copy-start.2
  21.6 0.0 collective-permute-done.3.refs_1_
  21.6 0.0 copy-start.3
  21.6 0.0 copy-done
  21.6 0.0 copy-done.1
  21.6 0.6 %copy-done.2 = bf16[4,8,2176]{2,1,0:T(8,128)(2,1)} copy-done((bf16[4,8,2176]{2,1,0:T(8,128)(2,1)}, bf16[4,8,2176]{2,1,0:T(8,128)(2,1)S(1)}, u32[]{:S(2)}) %copy-start.2) | copy-done | bytes 139288
  22.2 0.1 copy-done.3
  22.3 9.2 %project.1 = f32[2,4,2048]{2,1,0:T(4,128)} custom-call(s32[1]{0:T(128)} %bitcast.here_ref, s32[16]{0:T(128)} %constant.8.clone.order_ref, s32[32]{0:T(128)} %shift_ref.1, bf16[4,8,2176]{2,1,0:T(8,128)(2,1)} %copy-done, bf16[4,8,2176]{2,1,0:T(8,128)(2,1)} %copy-done.3, bf16[4,8,2176]{2,1,0:T(8,128)(2,1)} %copy-done.2, bf16[4,8,2176]{2,1,0:T(8,128)(2,1)} %copy-done.1), custom_call_target="tpu_custom_call" | custom-call | tf_op jit(solution)/shard_map/project/pallas_call | solution.py:209
Async XLA Ops:
  2.3 7.2 %collective-permute-start.2 = (bf16[1,8,2176]{2,1,0:T(8,128)(2,1)}, bf16[1,8,2176]{2,1,0:T(8,128)(2,1)S(1)}, u32[]{:S(2)}, u32[]{:S(2)}) collective-permute-start(bf16[1,8,2176]{2,1,0:T(8,128)(2,1)} %bitcast.3), channel_id=1, source_target_pairs={{0,24},{2,26},{4,28},{6,30},{8,16},{10,18},{12,20},{14,22},{16,8},... | collective-permute-start | bytes 104456 | tf_op jit(solution)/shard_map/ppermute | solution.py:179
  7.4 5.0 %collective-permute-start.1 = (bf16[1,8,2176]{2,1,0:T(8,128)(2,1)}, bf16[1,8,2176]{2,1,0:T(8,128)(2,1)S(1)}, u32[]{:S(2)}, u32[]{:S(2)}) collective-permute-start(bf16[1,8,2176]{2,1,0:T(8,128)(2,1)} %bitcast.4), channel_id=1, source_target_pairs={{0,16},{2,18},{4,20},{6,22},{8,24},{10,26},{12,28},{14,30},{16,0},... | collective-permute-start | bytes 104456 | tf_op jit(solution)/shard_map/ppermute | solution.py:179
  7.4 5.0 %collective-permute-start = (bf16[1,8,2176]{2,1,0:T(8,128)(2,1)}, bf16[1,8,2176]{2,1,0:T(8,128)(2,1)S(1)}, u32[]{:S(2)}, u32[]{:S(2)}) collective-permute-start(bf16[1,8,2176]{2,1,0:T(8,128)(2,1)} %bitcast.5), channel_id=1, source_target_pairs={{0,8},{2,10},{4,12},{6,14},{8,0},{10,2},{12,4},{14,6},{16,24},{18,... | collective-permute-start | bytes 104456 | tf_op jit(solution)/shard_map/ppermute | solution.py:179
  13.3 8.3 %copy-start = (bf16[4,8,2176]{2,1,0:T(8,128)(2,1)}, bf16[4,8,2176]{2,1,0:T(8,128)(2,1)S(1)}, u32[]{:S(2)}) copy-start(bf16[4,8,2176]{2,1,0:T(8,128)(2,1)S(1)} %pad_maximum_fusion.refs_0_) | copy-start | bytes 417796
  13.3 7.5 %collective-permute-start.5 = (bf16[4,8,2176]{2,1,0:T(8,128)(2,1)S(1)}, bf16[4,8,2176]{2,1,0:T(8,128)(2,1)S(1)}, u32[]{:S(2)}, u32[]{:S(2)}) collective-permute-start(bf16[4,8,2176]{2,1,0:T(8,128)(2,1)S(1)} %pad_maximum_fusion.refs_0_), channel_id=1, source_target_pairs={{0,6},{2,4},{4,2},{6,0},{8,14},{10,12},{12,10},{14,8},{16,22},{18,... | collective-permute-start | bytes 417800 | tf_op jit(solution)/shard_map/ppermute | solution.py:179
  15.8 5.8 %collective-permute-start.4 = (bf16[4,8,2176]{2,1,0:T(8,128)(2,1)S(1)}, bf16[4,8,2176]{2,1,0:T(8,128)(2,1)S(1)}, u32[]{:S(2)}, u32[]{:S(2)}) collective-permute-start(bf16[4,8,2176]{2,1,0:T(8,128)(2,1)S(1)} %pad_maximum_fusion.refs_0_), channel_id=1, source_target_pairs={{0,4},{2,6},{4,0},{6,2},{8,12},{10,14},{12,8},{14,10},{16,20},{18,... | collective-permute-start | bytes 417800 | tf_op jit(solution)/shard_map/ppermute | solution.py:179
  16.3 5.3 %collective-permute-start.3 = (bf16[4,8,2176]{2,1,0:T(8,128)(2,1)S(1)}, bf16[4,8,2176]{2,1,0:T(8,128)(2,1)S(1)}, u32[]{:S(2)}, u32[]{:S(2)}) collective-permute-start(bf16[4,8,2176]{2,1,0:T(8,128)(2,1)S(1)} %pad_maximum_fusion.refs_0_), channel_id=1, source_target_pairs={{0,2},{2,0},{4,6},{6,4},{8,10},{10,8},{12,14},{14,12},{16,18},{18,... | collective-permute-start | bytes 417800 | tf_op jit(solution)/shard_map/ppermute | solution.py:179
  20.8 0.8 %copy-start.1 = (bf16[4,8,2176]{2,1,0:T(8,128)(2,1)}, bf16[4,8,2176]{2,1,0:T(8,128)(2,1)S(1)}, u32[]{:S(2)}) copy-start(bf16[4,8,2176]{2,1,0:T(8,128)(2,1)S(1)} %collective-permute-done.5.refs_3_) | copy-start | bytes 417796
  21.6 0.7 %copy-start.2 = (bf16[4,8,2176]{2,1,0:T(8,128)(2,1)}, bf16[4,8,2176]{2,1,0:T(8,128)(2,1)S(1)}, u32[]{:S(2)}) copy-start(bf16[4,8,2176]{2,1,0:T(8,128)(2,1)S(1)} %collective-permute-done.4.refs_2_) | copy-start | bytes 417796
  21.6 0.7 %copy-start.3 = (bf16[4,8,2176]{2,1,0:T(8,128)(2,1)}, bf16[4,8,2176]{2,1,0:T(8,128)(2,1)S(1)}, u32[]{:S(2)}) copy-start(bf16[4,8,2176]{2,1,0:T(8,128)(2,1)S(1)} %collective-permute-done.3.refs_1_) | copy-start | bytes 417796

commit v3 on v2

--- a/solution.py
+++ b/solution.py
@@ -63,15 +63,14 @@
     )
 
 
-def project_kernel(here_ref, order_ref, shift_ref, *refs, pieces, nrows, bins, slices):
-    piece_refs, out_ref = refs[:pieces], refs[pieces]
-    val_ref, dif_ref, jit_ref, cos_ref, off_ref, low_ref = refs[pieces + 1 : pieces + 7]
-    tile_vmem, tile_smem, sem = refs[pieces + 7 :]
-    width = sum(ref.shape[0] for ref in piece_refs)
+def project(
+    here, order_ref, shift_ref, pieces, at, scratch, spread, emit, *, width, bins, slices
+):
+    val_ref, dif_ref, cos_ref, off_ref, low_ref, tile_vmem, tile_smem, sem = scratch
     angles = 2 * width
+    nrows = ROWS_DEV * width
     tiles = bins // LANES
     padded = tiles + 2
-    here = here_ref[0]
     lane = lax.broadcasted_iota(jnp.int32, (8, LANES), 1)
     sub = lax.broadcasted_iota(jnp.int32, (8, LANES), 0)
     first_half = sub < slices
@@ -85,46 +84,28 @@
         other = pltpu.roll(x, slices, axis=0)
         return jnp.where(first_half, x, other), jnp.where(first_half, other, x)
 
-    def spread_jitter(i, carry, piece, at):
-        one, two = both(piece[i, :, bins:].astype(jnp.float32))
-        d = here ^ order_ref[at + i]
-        jit_ref[2 * d] = one
-        jit_ref[2 * d + 1] = two
-        return carry
-
-    def each_device(function):
-        at = 0
-        for piece in piece_refs:
-            count = piece.shape[0]
-            lax.fori_loop(0, count, functools.partial(function, piece=piece, at=at), 0)
-            at += count
-
-    each_device(spread_jitter)
-
-    def prepare(i, carry, piece, at):
-        d = here ^ order_ref[at + i]
+    def prepare(i, carry, piece, first):
+        d = here ^ order_ref[at + first + i]
         raw = piece[i, :, bins:].astype(jnp.float32)
+        for p, jitter in enumerate(both(raw)):
+            spread(d, p, first + i, jitter)
         position = (2 * d).astype(jnp.float32) + jnp.where(first_half, 0.0, 1.0)
         theta = (position + raw) * math.pi / angles
         cosines = both(jnp.cos(theta))
         sines = both(jnp.sin(theta))
-        scales = []
+        local = 2 * (first + i)
         for p in range(2):
-            a = 2 * d + p
-            after = jit_ref[lax.rem(a + 1, angles)]
-            before = jit_ref[lax.rem(a + angles - 1, angles)]
-            scales.append((1.0 + (after - before) * 1.5) * (4.0 / math.sqrt(angles)))
             c, s = cosines[p], sines[p]
-            center = half + LANES + shift_ref[a].astype(jnp.float32)
+            center = half + LANES + shift_ref[2 * d + p].astype(jnp.float32)
             off = row_pos * s + center
             low = (jnp.where(c < 0, LANES - 1.0, 0.0) - half) * c + off
-            cos_ref[a] = c
-            off_ref[a] = (lane_f - half) * c + off
-            low_ref[a] = low
+            cos_ref[local + p] = c
+            off_ref[local + p] = (lane_f - half) * c + off
+            low_ref[local + p] = low
             lowest = low + c * (lane_f * LANES)
             lowest = jnp.minimum(lowest, pltpu.roll(lowest, slices, axis=0))
             first_tile = jnp.clip(lowest.astype(jnp.int32) >> 7, 0, padded - 2)
-            tile_vmem[pl.ds(a, 1), :] = first_tile[0:1, :]
+            tile_vmem[pl.ds(local + p, 1), :] = first_tile[0:1, :]
         zero = jnp.zeros((8, LANES), jnp.float32)
         current, moved = zero, zero
         for t in range(padded):
@@ -137,12 +118,16 @@
             values = both(current) if 0 < t < padded - 1 else (zero, zero)
             steps = both(step)
             for p in range(2):
-                val_ref[(2 * d + p) * padded + t] = values[p] * scales[p]
-                dif_ref[(2 * d + p) * padded + t] = steps[p] * scales[p]
+                val_ref[(local + p) * padded + t] = values[p]
+                dif_ref[(local + p) * padded + t] = steps[p]
             current, moved = following, following_moved
         return carry
 
-    each_device(prepare)
+    first = 0
+    for piece in pieces:
+        count = piece.shape[0]
+        lax.fori_loop(0, count, functools.partial(prepare, piece=piece, first=first), 0)
+        first += count
     copy = pltpu.make_async_copy(tile_vmem, tile_smem, sem)
     copy.start()
     copy.wait()
@@ -151,10 +136,10 @@
         c = cos_ref[a]
         start = off_ref[a]
         low = low_ref[a]
-        result = []
+        blocks = []
         for j in range(tiles):
             t = tile_smem[a, j]
-            at = a * padded + t
+            base = a * padded + t
             along = c * float(j * LANES)
             coord = start + along
             bottom = (low + along).astype(jnp.int32)
@@ -162,16 +147,87 @@
             frac = coord - lower.astype(jnp.float32)
             near = lane >= bottom - t * LANES
             inner = lower & (LANES - 1)
-            value = lane_take(jnp.where(near, val_ref[at], val_ref[at + 1]), inner)
-            step = lane_take(jnp.where(near, dif_ref[at], dif_ref[at + 1]), inner)
-            result.append(accum[j] + (value + frac * step))
-        return tuple(result)
-
-    init = tuple(jnp.zeros((8, LANES), jnp.float32) for _ in range(tiles))
-    accum = lax.fori_loop(0, angles, one_angle, init)
+            value = lane_take(jnp.where(near, val_ref[base], val_ref[base + 1]), inner)
+            step = lane_take(jnp.where(near, dif_ref[base], dif_ref[base + 1]), inner)
+            blocks.append(value + frac * step)
+        return emit(a, blocks, accum)
+
+    return one_angle, 2 * first
+
+
+def early_kernel(here_ref, order_ref, shift_ref, held_ref, rows_ref, jit_ref, *scratch, width, bins, slices):
+    tiles = bins // LANES
+
+    def spread(d, p, local, jitter):
+        jit_ref[2 * local + p] = jitter
+
+    def emit(a, blocks, carry):
+        for j in range(tiles):
+            rows_ref[a * tiles + j] = blocks[j]
+        return carry
+
+    one_angle, count = project(
+        here_ref[0], order_ref, shift_ref, [held_ref], 0, scratch, spread, emit,
+        width=width, bins=bins, slices=slices,
+    )
+    lax.fori_loop(0, count, one_angle, 0)
+
+
+def late_kernel(here_ref, order_ref, shift_ref, rows_ref, held_jit_ref, *refs, pieces, width, bins, slices):
+    piece_refs, out_ref, jit_ref, scratch = (
+        refs[:pieces], refs[pieces], refs[pieces + 1], refs[pieces + 2 :]
+    )
+    here = here_ref[0]
+    angles = 2 * width
+    tiles = bins // LANES
+    held = held_jit_ref.shape[0] // 2
+
+    def weight(position, p):
+        a = 2 * (here ^ order_ref[position]) + p
+        after = jit_ref[lax.rem(a + 1, angles)]
+        before = jit_ref[lax.rem(a + angles - 1, angles)]
+        return (1.0 + (after - before) * 1.5) * (4.0 / math.sqrt(angles))
+
+    def spread(d, p, local, jitter):
+        jit_ref[2 * d + p] = jitter
+
+    def emit(a, blocks, accum):
+        scale = weight(held + (a >> 1), a & 1)
+        return tuple(accum[j] + scale * blocks[j] for j in range(tiles))
+
+    for i in range(held):
+        d = here ^ order_ref[i]
+        for p in range(2):
+            jit_ref[2 * d + p] = held_jit_ref[2 * i + p]
+    one_angle, count = project(
+        here, order_ref, shift_ref, piece_refs, held, scratch, spread, emit,
+        width=width, bins=bins, slices=slices,
+    )
+
+    def add_early(a, accum):
+        scale = weight(a >> 1, a & 1)
+        return tuple(accum[j] + scale * rows_ref[a * tiles + j] for j in range(tiles))
+
+    accum = tuple(jnp.zeros((8, LANES), jnp.float32) for _ in range(tiles))
+    accum = lax.fori_loop(0, 2 * held, add_early, accum)
+    accum = lax.fori_loop(0, count, one_angle, accum)
     for j in range(tiles):
         for r in range(ROWS_DEV):
             out_ref[r, :, j * LANES : (j + 1) * LANES] = accum[j][r * slices : (r + 1) * slices]
+
+
+def working_set(count, bins):
+    blocks = (bins // LANES + 2) * count
+    return [
+        pltpu.VMEM((blocks, 8, LANES), jnp.float32),
+        pltpu.VMEM((blocks, 8, LANES), jnp.float32),
+        pltpu.VMEM((count, 8, LANES), jnp.float32),
+        pltpu.VMEM((count, 8, LANES), jnp.float32),
+        pltpu.VMEM((count, 8, LANES), jnp.float32),
+        pltpu.VMEM((count, LANES), jnp.int32),
+        pltpu.SMEM((count, LANES), jnp.int32),
+        pltpu.SemaphoreType.DMA(()),
+    ]
 
 
 def exchange(pieces, width, stride, group):
@@ -185,8 +241,6 @@
     ang_dev, slices, bins = sinogram.shape
     width = lax.axis_size("blk")
     angles = width * ang_dev
-    nrows = ROWS_DEV * width
-    padded = bins // LANES + 2
     here = lax.axis_index("blk").astype(jnp.int32).reshape(1)
     payload = pl.pallas_call(
         filter_kernel,
@@ -206,28 +260,29 @@
         order = [o ^ (k * stride) for k in range(group) for o in order]
         pieces = [held] + exchange(held, width, stride, group)
     order = jnp.asarray(order, jnp.int32)
+    held, rest = pieces[0], pieces[1:]
+    early = 2 * held.shape[0]
+    late = angles - early
+    scalars = [pl.BlockSpec(memory_space=pltpu.SMEM)] * 3
+    whole = pl.BlockSpec(memory_space=pltpu.VMEM)
+    rows, held_jitter = pl.pallas_call(
+        functools.partial(early_kernel, width=width, bins=bins, slices=slices),
+        in_specs=scalars + [whole],
+        out_specs=[whole, whole],
+        out_shape=[
+            jax.ShapeDtypeStruct((early * (bins // LANES), 8, LANES), jnp.float32),
+            jax.ShapeDtypeStruct((early, 8, LANES), jnp.float32),
+        ],
+        scratch_shapes=working_set(early, bins),
+        name="early",
+    )(here, order, shift, held)
     return pl.pallas_call(
-        functools.partial(project_kernel, pieces=len(pieces), nrows=nrows, bins=bins, slices=slices),
-        in_specs=[
-            pl.BlockSpec(memory_space=pltpu.SMEM),
-            pl.BlockSpec(memory_space=pltpu.SMEM),
-            pl.BlockSpec(memory_space=pltpu.SMEM),
-        ]
-        + [pl.BlockSpec(memory_space=pltpu.VMEM)] * len(pieces),
+        functools.partial(late_kernel, pieces=len(rest), width=width, bins=bins, slices=slices),
+        in_specs=scalars + [whole] * (2 + len(rest)),
         out_shape=jax.ShapeDtypeStruct((ROWS_DEV, slices, bins), jnp.float32),
-        scratch_shapes=[
-            pltpu.VMEM((angles * padded, 8, LANES), jnp.float32),
-            pltpu.VMEM((angles * padded, 8, LANES), jnp.float32),
-            pltpu.VMEM((angles, 8, LANES), jnp.float32),
-            pltpu.VMEM((angles, 8, LANES), jnp.float32),
-            pltpu.VMEM((angles, 8, LANES), jnp.float32),
-            pltpu.VMEM((angles, 8, LANES), jnp.float32),
-            pltpu.VMEM((angles, LANES), jnp.int32),
-            pltpu.SMEM((angles, LANES), jnp.int32),
-            pltpu.SemaphoreType.DMA(()),
-        ],
-        name="project",
-    )(here, order, shift, *pieces)
+        scratch_shapes=[pltpu.VMEM((angles, 8, LANES), jnp.float32)] + working_set(late, bins),
+        name="late",
+    )(here, order, shift, rows, held_jitter, *rest)
 
 
 def solution(mesh):

time: 31.7 us -> 30.1 us (0.950)
  waiting for transfers between devices: 9.21 us -> 5.3 us
  Pallas kernels: 11.5 us -> 13.8 us
    ppermute x6, waiting for transfers between devices: 9.21 us -> 5.3 us  [exchange(): lax.ppermute(pieces, 'blk', [(i, i ^ k * stride) for i in range(width)])]
    pallas_call x1 -> x2, Pallas kernels: 9.15 us -> 11.5 us  [the longest x1 7.57 us: body(): pl.pallas_call(functools.partial(late_kernel, pieces=len(rest), width=wid...]
  transfers between devices with their start and end apart: 6 -> 6, of which waited for: 4 -> 3; matrix products, arithmetic and copies ran while one was open for 0% -> 0% of each run, Pallas kernels for 0% -> 13%
where the time goes in v3:
time: 30.1 us; the launch traced here: 29.8 us
  Pallas kernels  13.8 us (46%)
  starting transfers between devices  9.2 us (31%)
  waiting for transfers between devices  5.3 us (18%)
  other arithmetic  0.79 us (3%)
  local copies, waits for them, and re-layouts  0.71 us (2%)
    ppermute x6, starting transfers between devices, exchange(): lax.ppermute(pieces, 'blk', [(i, i ^ k * stride) for i in range(width)])  9.2 us
    pallas_call x1, Pallas kernels, body(): pl.pallas_call(functools.partial(late_kernel, pieces=len(rest), width=wid...  7.57 us
    ppermute x6, waiting for transfers between devices, exchange(): lax.ppermute(pieces, 'blk', [(i, i ^ k * stride) for i in range(width)])  5.3 us
    pallas_call x1, Pallas kernels, body(): pl.pallas_call(functools.partial(early_kernel, width=width, bins=bins, sl...  3.9 us
    pallas_call x1, Pallas kernels, body(): pl.pallas_call(filter_kernel, out_shape=jax.ShapeDtypeStruct((ang_dev * s...  2.34 us
    concatenate x1, other arithmetic, body(): held = pieces[0] if len(pieces) == 1 else jnp.concatenate(pieces, axis=0)  0.79 us
    unnamed x8, local copies, waits for them, and re-layouts  0.71 us
  transfers between devices with their start and end apart: 6, of which 3 were waited for; matrix products, arithmetic and copies ran while one was open for 0% of the time, Pallas kernels for 13%

profile of v3, /device:TPU:0, one launch (start us, length us, event | category | flops | bytes accessed | tf_op | source)
XLA Modules:
  0.0 29.8 jit_solution(11271275110798314690)
XLA Ops:
  0.0 2.3 %filter.1 = bf16[8,2176]{1,0:T(8,128)(2,1)} custom-call(bf16[2,4,2048]{2,1,0:T(4,128)(2,1)} %sino_ref.1, bf16[1,2]{1,0:T(2,128)(2,1)} %bitcast.7), custom_call_target="tpu_custom_call" | custom-call | tf_op jit(solution)/shard_map/filter/pallas_call | solution.py:245
  2.3 5.1 %collective-permute-start.2 = (bf16[1,8,2176]{2,1,0:T(8,128)(2,1)}, bf16[1,8,2176]{2,1,0:T(8,128)(2,1)S(1)}, u32[]{:S(2)}, u32[]{:S(2)}) collective-permute-start(bf16[1,8,2176]{2,1,0:T(8,128)(2,1)} %bitcast.3), channel_id=1, source_target_pairs={{0,24},{2,26},{4,28},{6,30},{8,16},{10,18},{12,20},{14,22},{16,8},... | collective-permute-start | bytes 104456 | tf_op jit(solution)/shard_map/ppermute | solution.py:235
  7.4 0.0 collective-permute-start.1
  7.4 0.6 %collective-permute-start = (bf16[1,8,2176]{2,1,0:T(8,128)(2,1)}, bf16[1,8,2176]{2,1,0:T(8,128)(2,1)S(1)}, u32[]{:S(2)}, u32[]{:S(2)}) collective-permute-start(bf16[1,8,2176]{2,1,0:T(8,128)(2,1)} %bitcast.5), channel_id=1, source_target_pairs={{0,8},{2,10},{4,12},{6,14},{8,0},{10,2},{12,4},{14,6},{16,24},{18,... | collective-permute-start | bytes 104456 | tf_op jit(solution)/shard_map/ppermute | solution.py:235
  8.0 1.6 %collective-permute-done.2 = bf16[1,8,2176]{2,1,0:T(8,128)(2,1)S(1)} collective-permute-done((bf16[1,8,2176]{2,1,0:T(8,128)(2,1)}, bf16[1,8,2176]{2,1,0:T(8,128)(2,1)S(1)}, u32[]{:S(2)}, u32[]{:S(2)}) %collective-permute-start.2) | collective-permute-done | bytes 34848 | tf_op jit(solution)/shard_map/ppermute | solution.py:235
  9.5 2.9 %collective-permute-done.1 = bf16[1,8,2176]{2,1,0:T(8,128)(2,1)S(1)} collective-permute-done((bf16[1,8,2176]{2,1,0:T(8,128)(2,1)}, bf16[1,8,2176]{2,1,0:T(8,128)(2,1)S(1)}, u32[]{:S(2)}, u32[]{:S(2)}) %collective-permute-start.1) | collective-permute-done | bytes 34848 | tf_op jit(solution)/shard_map/ppermute | solution.py:235
  12.5 0.0 collective-permute-done
  12.5 0.8 %pad_maximum_fusion.held_ref = bf16[4,8,2176]{2,1,0:T(8,128)(2,1)S(1)} fusion(bf16[1,8,2176]{2,1,0:T(8,128)(2,1)S(1)} %collective-permute-done.2, bf16[1,8,2176]{2,1,0:T(8,128)(2,1)S(1)} %collective-permute-done.1, bf16[1,8,2176]{2,1,0:T(8,128)(2,1)S(1)} %collective-permute-done, bf16[1,8,2176]{2,1,0:T(8,128)(2,1)} %bitcast.6), kind=kLoop, calls=%fused_computation | loop fusion | flops 208896 | bytes 278528 | tf_op jit(solution)/shard_map/concatenate | solution.py:259
  13.3 0.0 copy-start
  13.3 2.5 %collective-permute-start.5 = (bf16[4,8,2176]{2,1,0:T(8,128)(2,1)S(1)}, bf16[4,8,2176]{2,1,0:T(8,128)(2,1)S(1)}, u32[]{:S(2)}, u32[]{:S(2)}) collective-permute-start(bf16[4,8,2176]{2,1,0:T(8,128)(2,1)S(1)} %pad_maximum_fusion.held_ref), channel_id=1, source_target_pairs={{0,6},{2,4},{4,2},{6,0},{8,14},{10,12},{12,10},{14,8},{16,22},{18,... | collective-permute-start | bytes 417800 | tf_op jit(solution)/shard_map/ppermute | solution.py:235
  15.8 0.5 %collective-permute-start.4 = (bf16[4,8,2176]{2,1,0:T(8,128)(2,1)S(1)}, bf16[4,8,2176]{2,1,0:T(8,128)(2,1)S(1)}, u32[]{:S(2)}, u32[]{:S(2)}) collective-permute-start(bf16[4,8,2176]{2,1,0:T(8,128)(2,1)S(1)} %pad_maximum_fusion.held_ref), channel_id=1, source_target_pairs={{0,4},{2,6},{4,0},{6,2},{8,12},{10,14},{12,8},{14,10},{16,20},{18,... | collective-permute-start | bytes 417800 | tf_op jit(solution)/shard_map/ppermute | solution.py:235
  16.3 0.5 %collective-permute-start.3 = (bf16[4,8,2176]{2,1,0:T(8,128)(2,1)S(1)}, bf16[4,8,2176]{2,1,0:T(8,128)(2,1)S(1)}, u32[]{:S(2)}, u32[]{:S(2)}) collective-permute-start(bf16[4,8,2176]{2,1,0:T(8,128)(2,1)S(1)} %pad_maximum_fusion.held_ref), channel_id=1, source_target_pairs={{0,2},{2,0},{4,6},{6,4},{8,10},{10,8},{12,14},{14,12},{16,18},{18,... | collective-permute-start | bytes 417800 | tf_op jit(solution)/shard_map/ppermute | solution.py:235
  16.8 0.0 copy-done
  16.8 3.9 %early.1 = (f32[128,8,128]{2,1,0:T(8,128)}, f32[8,8,128]{2,1,0:T(8,128)}) custom-call(s32[1]{0:T(128)} %bitcast.here_ref, s32[16]{0:T(128)} %constant.8.clone.order_ref, s32[32]{0:T(128)} %shift_ref.3, bf16[4,8,2176]{2,1,0:T(8,128)(2,1)} %copy-done), custom_call_target="tpu_custom_call" | custom-call | tf_op jit(solution)/shard_map/early/pallas_call | solution.py:268
  20.7 0.0 collective-permute-done.5.refs_2_
  20.8 0.0 copy-start.1
  20.8 0.8 %collective-permute-done.4.refs_1_ = bf16[4,8,2176]{2,1,0:T(8,128)(2,1)S(1)} collective-permute-done((bf16[4,8,2176]{2,1,0:T(8,128)(2,1)S(1)}, bf16[4,8,2176]{2,1,0:T(8,128)(2,1)S(1)}, u32[]{:S(2)}, u32[]{:S(2)}) %collective-permute-start.4) | collective-permute-done | bytes 139296 | tf_op jit(solution)/shard_map/ppermute | solution.py:235
  21.6 0.0 copy-start.2
  21.6 0.0 collective-permute-done.3.refs_0_
  21.6 0.0 copy-start.3
  21.6 0.0 copy-done.1
  21.6 0.6 %copy-done.2 = bf16[4,8,2176]{2,1,0:T(8,128)(2,1)} copy-done((bf16[4,8,2176]{2,1,0:T(8,128)(2,1)}, bf16[4,8,2176]{2,1,0:T(8,128)(2,1)S(1)}, u32[]{:S(2)}) %copy-start.2) | copy-done | bytes 139288
  22.2 0.1 copy-done.3
  22.3 7.6 %late.1 = f32[2,4,2048]{2,1,0:T(4,128)} custom-call(s32[1]{0:T(128)} %bitcast.here_ref, s32[16]{0:T(128)} %constant.8.clone.order_ref, s32[32]{0:T(128)} %shift_ref.3, f32[128,8,128]{2,1,0:T(8,128)} %get-tuple-element.7.rows_ref, f32[8,8,128]{2,1,0:T(8,128)} %get-tuple-element.8.held_jit_ref, bf16[4,8,2176]{2,1,0:T(8,128)(2,1)} %copy-done.3, ...), custom_call_target="tpu_custom_call" | custom-call | tf_op jit(solution)/shard_map/late/pallas_call | solution.py:279
Async XLA Ops:
  2.3 7.2 %collective-permute-start.2 = (bf16[1,8,2176]{2,1,0:T(8,128)(2,1)}, bf16[1,8,2176]{2,1,0:T(8,128)(2,1)S(1)}, u32[]{:S(2)}, u32[]{:S(2)}) collective-permute-start(bf16[1,8,2176]{2,1,0:T(8,128)(2,1)} %bitcast.3), channel_id=1, source_target_pairs={{0,24},{2,26},{4,28},{6,30},{8,16},{10,18},{12,20},{14,22},{16,8},... | collective-permute-start | bytes 104456 | tf_op jit(solution)/shard_map/ppermute | solution.py:235
  7.4 5.0 %collective-permute-start.1 = (bf16[1,8,2176]{2,1,0:T(8,128)(2,1)}, bf16[1,8,2176]{2,1,0:T(8,128)(2,1)S(1)}, u32[]{:S(2)}, u32[]{:S(2)}) collective-permute-start(bf16[1,8,2176]{2,1,0:T(8,128)(2,1)} %bitcast.4), channel_id=1, source_target_pairs={{0,16},{2,18},{4,20},{6,22},{8,24},{10,26},{12,28},{14,30},{16,0},... | collective-permute-start | bytes 104456 | tf_op jit(solution)/shard_map/ppermute | solution.py:235
  7.4 5.0 %collective-permute-start = (bf16[1,8,2176]{2,1,0:T(8,128)(2,1)}, bf16[1,8,2176]{2,1,0:T(8,128)(2,1)S(1)}, u32[]{:S(2)}, u32[]{:S(2)}) collective-permute-start(bf16[1,8,2176]{2,1,0:T(8,128)(2,1)} %bitcast.5), channel_id=1, source_target_pairs={{0,8},{2,10},{4,12},{6,14},{8,0},{10,2},{12,4},{14,6},{16,24},{18,... | collective-permute-start | bytes 104456 | tf_op jit(solution)/shard_map/ppermute | solution.py:235
  13.3 3.6 %copy-start = (bf16[4,8,2176]{2,1,0:T(8,128)(2,1)}, bf16[4,8,2176]{2,1,0:T(8,128)(2,1)S(1)}, u32[]{:S(2)}) copy-start(bf16[4,8,2176]{2,1,0:T(8,128)(2,1)S(1)} %pad_maximum_fusion.held_ref) | copy-start | bytes 417796
  13.3 7.5 %collective-permute-start.5 = (bf16[4,8,2176]{2,1,0:T(8,128)(2,1)S(1)}, bf16[4,8,2176]{2,1,0:T(8,128)(2,1)S(1)}, u32[]{:S(2)}, u32[]{:S(2)}) collective-permute-start(bf16[4,8,2176]{2,1,0:T(8,128)(2,1)S(1)} %pad_maximum_fusion.held_ref), channel_id=1, source_target_pairs={{0,6},{2,4},{4,2},{6,0},{8,14},{10,12},{12,10},{14,8},{16,22},{18,... | collective-permute-start | bytes 417800 | tf_op jit(solution)/shard_map/ppermute | solution.py:235
  15.8 5.8 %collective-permute-start.4 = (bf16[4,8,2176]{2,1,0:T(8,128)(2,1)S(1)}, bf16[4,8,2176]{2,1,0:T(8,128)(2,1)S(1)}, u32[]{:S(2)}, u32[]{:S(2)}) collective-permute-start(bf16[4,8,2176]{2,1,0:T(8,128)(2,1)S(1)} %pad_maximum_fusion.held_ref), channel_id=1, source_target_pairs={{0,4},{2,6},{4,0},{6,2},{8,12},{10,14},{12,8},{14,10},{16,20},{18,... | collective-permute-start | bytes 417800 | tf_op jit(solution)/shard_map/ppermute | solution.py:235
  16.3 5.3 %collective-permute-start.3 = (bf16[4,8,2176]{2,1,0:T(8,128)(2,1)S(1)}, bf16[4,8,2176]{2,1,0:T(8,128)(2,1)S(1)}, u32[]{:S(2)}, u32[]{:S(2)}) collective-permute-start(bf16[4,8,2176]{2,1,0:T(8,128)(2,1)S(1)} %pad_maximum_fusion.held_ref), channel_id=1, source_target_pairs={{0,2},{2,0},{4,6},{6,4},{8,10},{10,8},{12,14},{14,12},{16,18},{18,... | collective-permute-start | bytes 417800 | tf_op jit(solution)/shard_map/ppermute | solution.py:235
  20.8 0.8 %copy-start.1 = (bf16[4,8,2176]{2,1,0:T(8,128)(2,1)}, bf16[4,8,2176]{2,1,0:T(8,128)(2,1)S(1)}, u32[]{:S(2)}) copy-start(bf16[4,8,2176]{2,1,0:T(8,128)(2,1)S(1)} %collective-permute-done.5.refs_2_) | copy-start | bytes 417796
  21.6 0.7 %copy-start.2 = (bf16[4,8,2176]{2,1,0:T(8,128)(2,1)}, bf16[4,8,2176]{2,1,0:T(8,128)(2,1)S(1)}, u32[]{:S(2)}) copy-start(bf16[4,8,2176]{2,1,0:T(8,128)(2,1)S(1)} %collective-permute-done.4.refs_1_) | copy-start | bytes 417796
  21.6 0.7 %copy-start.3 = (bf16[4,8,2176]{2,1,0:T(8,128)(2,1)}, bf16[4,8,2176]{2,1,0:T(8,128)(2,1)S(1)}, u32[]{:S(2)}) copy-start(bf16[4,8,2176]{2,1,0:T(8,128)(2,1)S(1)} %collective-permute-done.3.refs_0_) | copy-start | bytes 417796

commit v4 on v3

--- a/solution.py
+++ b/solution.py
@@ -126,7 +126,7 @@
     first = 0
     for piece in pieces:
         count = piece.shape[0]
-        lax.fori_loop(0, count, functools.partial(prepare, piece=piece, first=first), 0)
+        lax.fori_loop(0, count, functools.partial(prepare, piece=piece, first=first), 0, unroll=2)
         first += count
     copy = pltpu.make_async_copy(tile_vmem, tile_smem, sem)
     copy.start()
@@ -170,7 +170,7 @@
         here_ref[0], order_ref, shift_ref, [held_ref], 0, scratch, spread, emit,
         width=width, bins=bins, slices=slices,
     )
-    lax.fori_loop(0, count, one_angle, 0)
+    lax.fori_loop(0, count, one_angle, 0, unroll=4)
 
 
 def late_kernel(here_ref, order_ref, shift_ref, rows_ref, held_jit_ref, *refs, pieces, width, bins, slices):
@@ -210,7 +210,7 @@
 
     accum = tuple(jnp.zeros((8, LANES), jnp.float32) for _ in range(tiles))
     accum = lax.fori_loop(0, 2 * held, add_early, accum)
-    accum = lax.fori_loop(0, count, one_angle, accum)
+    accum = lax.fori_loop(0, count, one_angle, accum, unroll=4)
     for j in range(tiles):
         for r in range(ROWS_DEV):
             out_ref[r, :, j * LANES : (j + 1) * LANES] = accum[j][r * slices : (r + 1) * slices]

time: 30.1 us -> 28.3 us (0.940)
  Pallas kernels: 13.8 us -> 11.4 us
  waiting for transfers between devices: 5.3 us -> 5.89 us
    pallas_call x1, Pallas kernels: 7.57 us -> 5.74 us  [body(): pl.pallas_call(functools.partial(late_kernel, pieces=len(rest), width=wid...]
    ppermute x6, waiting for transfers between devices: 5.3 us -> 5.89 us  [exchange(): lax.ppermute(pieces, 'blk', [(i, i ^ k * stride) for i in range(width)])]
    pallas_call x1, Pallas kernels: 3.9 us -> 3.31 us  [body(): pl.pallas_call(functools.partial(early_kernel, width=width, bins=bins, sl...]
  transfers between devices with their start and end apart: 6 -> 6, of which waited for: 3 -> 4; matrix products, arithmetic and copies ran while one was open for 0% -> 0% of each run, Pallas kernels for 13% -> 12%
where the time goes in v4:
time: 28.3 us; the launch traced here: 28 us
  Pallas kernels  11.4 us (40%)
  starting transfers between devices  9.2 us (33%)
  waiting for transfers between devices  5.89 us (21%)
  other arithmetic  0.79 us (3%)
  local copies, waits for them, and re-layouts  0.71 us (3%)
    ppermute x6, starting transfers between devices, exchange(): lax.ppermute(pieces, 'blk', [(i, i ^ k * stride) for i in range(width)])  9.2 us
    ppermute x6, waiting for transfers between devices, exchange(): lax.ppermute(pieces, 'blk', [(i, i ^ k * stride) for i in range(width)])  5.89 us
    pallas_call x1, Pallas kernels, body(): pl.pallas_call(functools.partial(late_kernel, pieces=len(rest), width=wid...  5.74 us
    pallas_call x1, Pallas kernels, body(): pl.pallas_call(functools.partial(early_kernel, width=width, bins=bins, sl...  3.31 us
    pallas_call x1, Pallas kernels, body(): pl.pallas_call(filter_kernel, out_shape=jax.ShapeDtypeStruct((ang_dev * s...  2.34 us
    concatenate x1, other arithmetic, body(): held = pieces[0] if len(pieces) == 1 else jnp.concatenate(pieces, axis=0)  0.79 us
    unnamed x8, local copies, waits for them, and re-layouts  0.71 us
  transfers between devices with their start and end apart: 6, of which 4 were waited for; matrix products, arithmetic and copies ran while one was open for 0% of the time, Pallas kernels for 12%

profile of v4, /device:TPU:0, one launch (start us, length us, event | category | flops | bytes accessed | tf_op | source)
XLA Modules:
  0.0 28.0 jit_solution(13174350262834022129)
XLA Ops:
  0.0 2.3 %filter.1 = bf16[8,2176]{1,0:T(8,128)(2,1)} custom-call(bf16[2,4,2048]{2,1,0:T(4,128)(2,1)} %sino_ref.1, bf16[1,2]{1,0:T(2,128)(2,1)} %bitcast.7), custom_call_target="tpu_custom_call" | custom-call | tf_op jit(solution)/shard_map/filter/pallas_call | solution.py:245
  2.3 5.1 %collective-permute-start.2 = (bf16[1,8,2176]{2,1,0:T(8,128)(2,1)}, bf16[1,8,2176]{2,1,0:T(8,128)(2,1)S(1)}, u32[]{:S(2)}, u32[]{:S(2)}) collective-permute-start(bf16[1,8,2176]{2,1,0:T(8,128)(2,1)} %bitcast.3), channel_id=1, source_target_pairs={{0,24},{2,26},{4,28},{6,30},{8,16},{10,18},{12,20},{14,22},{16,8},... | collective-permute-start | bytes 104456 | tf_op jit(solution)/shard_map/ppermute | solution.py:235
  7.4 0.0 collective-permute-start.1
  7.4 0.6 %collective-permute-start = (bf16[1,8,2176]{2,1,0:T(8,128)(2,1)}, bf16[1,8,2176]{2,1,0:T(8,128)(2,1)S(1)}, u32[]{:S(2)}, u32[]{:S(2)}) collective-permute-start(bf16[1,8,2176]{2,1,0:T(8,128)(2,1)} %bitcast.5), channel_id=1, source_target_pairs={{0,8},{2,10},{4,12},{6,14},{8,0},{10,2},{12,4},{14,6},{16,24},{18,... | collective-permute-start | bytes 104456 | tf_op jit(solution)/shard_map/ppermute | solution.py:235
  8.0 1.6 %collective-permute-done.2 = bf16[1,8,2176]{2,1,0:T(8,128)(2,1)S(1)} collective-permute-done((bf16[1,8,2176]{2,1,0:T(8,128)(2,1)}, bf16[1,8,2176]{2,1,0:T(8,128)(2,1)S(1)}, u32[]{:S(2)}, u32[]{:S(2)}) %collective-permute-start.2) | collective-permute-done | bytes 34848 | tf_op jit(solution)/shard_map/ppermute | solution.py:235
  9.5 2.9 %collective-permute-done.1 = bf16[1,8,2176]{2,1,0:T(8,128)(2,1)S(1)} collective-permute-done((bf16[1,8,2176]{2,1,0:T(8,128)(2,1)}, bf16[1,8,2176]{2,1,0:T(8,128)(2,1)S(1)}, u32[]{:S(2)}, u32[]{:S(2)}) %collective-permute-start.1) | collective-permute-done | bytes 34848 | tf_op jit(solution)/shard_map/ppermute | solution.py:235
  12.5 0.0 collective-permute-done
  12.5 0.8 %pad_maximum_fusion.held_ref = bf16[4,8,2176]{2,1,0:T(8,128)(2,1)S(1)} fusion(bf16[1,8,2176]{2,1,0:T(8,128)(2,1)S(1)} %collective-permute-done.2, bf16[1,8,2176]{2,1,0:T(8,128)(2,1)S(1)} %collective-permute-done.1, bf16[1,8,2176]{2,1,0:T(8,128)(2,1)S(1)} %collective-permute-done, bf16[1,8,2176]{2,1,0:T(8,128)(2,1)} %bitcast.6), kind=kLoop, calls=%fused_computation | loop fusion | flops 208896 | bytes 278528 | tf_op jit(solution)/shard_map/concatenate | solution.py:259
  13.3 0.0 copy-start
  13.3 2.5 %collective-permute-start.5 = (bf16[4,8,2176]{2,1,0:T(8,128)(2,1)S(1)}, bf16[4,8,2176]{2,1,0:T(8,128)(2,1)S(1)}, u32[]{:S(2)}, u32[]{:S(2)}) collective-permute-start(bf16[4,8,2176]{2,1,0:T(8,128)(2,1)S(1)} %pad_maximum_fusion.held_ref), channel_id=1, source_target_pairs={{0,6},{2,4},{4,2},{6,0},{8,14},{10,12},{12,10},{14,8},{16,22},{18,... | collective-permute-start | bytes 417800 | tf_op jit(solution)/shard_map/ppermute | solution.py:235
  15.8 0.5 %collective-permute-start.4 = (bf16[4,8,2176]{2,1,0:T(8,128)(2,1)S(1)}, bf16[4,8,2176]{2,1,0:T(8,128)(2,1)S(1)}, u32[]{:S(2)}, u32[]{:S(2)}) collective-permute-start(bf16[4,8,2176]{2,1,0:T(8,128)(2,1)S(1)} %pad_maximum_fusion.held_ref), channel_id=1, source_target_pairs={{0,4},{2,6},{4,0},{6,2},{8,12},{10,14},{12,8},{14,10},{16,20},{18,... | collective-permute-start | bytes 417800 | tf_op jit(solution)/shard_map/ppermute | solution.py:235
  16.3 0.5 %collective-permute-start.3 = (bf16[4,8,2176]{2,1,0:T(8,128)(2,1)S(1)}, bf16[4,8,2176]{2,1,0:T(8,128)(2,1)S(1)}, u32[]{:S(2)}, u32[]{:S(2)}) collective-permute-start(bf16[4,8,2176]{2,1,0:T(8,128)(2,1)S(1)} %pad_maximum_fusion.held_ref), channel_id=1, source_target_pairs={{0,2},{2,0},{4,6},{6,4},{8,10},{10,8},{12,14},{14,12},{16,18},{18,... | collective-permute-start | bytes 417800 | tf_op jit(solution)/shard_map/ppermute | solution.py:235
  16.8 0.0 copy-done
  16.8 3.3 %early.1 = (f32[128,8,128]{2,1,0:T(8,128)}, f32[8,8,128]{2,1,0:T(8,128)}) custom-call(s32[1]{0:T(128)} %bitcast.here_ref, s32[16]{0:T(128)} %constant.8.clone.order_ref, s32[32]{0:T(128)} %shift_ref.3, bf16[4,8,2176]{2,1,0:T(8,128)(2,1)} %copy-done), custom_call_target="tpu_custom_call" | custom-call | tf_op jit(solution)/shard_map/early/pallas_call | solution.py:268
  20.2 0.6 %collective-permute-done.5.refs_2_ = bf16[4,8,2176]{2,1,0:T(8,128)(2,1)S(1)} collective-permute-done((bf16[4,8,2176]{2,1,0:T(8,128)(2,1)S(1)}, bf16[4,8,2176]{2,1,0:T(8,128)(2,1)S(1)}, u32[]{:S(2)}, u32[]{:S(2)}) %collective-permute-start.5) | collective-permute-done | bytes 139296 | tf_op jit(solution)/shard_map/ppermute | solution.py:235
  20.8 0.0 copy-start.1
  20.8 0.8 %collective-permute-done.4.refs_1_ = bf16[4,8,2176]{2,1,0:T(8,128)(2,1)S(1)} collective-permute-done((bf16[4,8,2176]{2,1,0:T(8,128)(2,1)S(1)}, bf16[4,8,2176]{2,1,0:T(8,128)(2,1)S(1)}, u32[]{:S(2)}, u32[]{:S(2)}) %collective-permute-start.4) | collective-permute-done | bytes 139296 | tf_op jit(solution)/shard_map/ppermute | solution.py:235
  21.6 0.0 copy-start.2
  21.6 0.0 collective-permute-done.3.refs_0_
  21.6 0.0 copy-start.3
  21.6 0.0 copy-done.1
  21.6 0.6 %copy-done.2 = bf16[4,8,2176]{2,1,0:T(8,128)(2,1)} copy-done((bf16[4,8,2176]{2,1,0:T(8,128)(2,1)}, bf16[4,8,2176]{2,1,0:T(8,128)(2,1)S(1)}, u32[]{:S(2)}) %copy-start.2) | copy-done | bytes 139288
  22.2 0.1 copy-done.3
  22.3 5.7 %late.1 = f32[2,4,2048]{2,1,0:T(4,128)} custom-call(s32[1]{0:T(128)} %bitcast.here_ref, s32[16]{0:T(128)} %constant.8.clone.order_ref, s32[32]{0:T(128)} %shift_ref.3, f32[128,8,128]{2,1,0:T(8,128)} %get-tuple-element.7.rows_ref, f32[8,8,128]{2,1,0:T(8,128)} %get-tuple-element.8.held_jit_ref, bf16[4,8,2176]{2,1,0:T(8,128)(2,1)} %copy-done.3, ...), custom_call_target="tpu_custom_call" | custom-call | tf_op jit(solution)/shard_map/late/pallas_call | solution.py:279
Async XLA Ops:
  2.3 7.2 %collective-permute-start.2 = (bf16[1,8,2176]{2,1,0:T(8,128)(2,1)}, bf16[1,8,2176]{2,1,0:T(8,128)(2,1)S(1)}, u32[]{:S(2)}, u32[]{:S(2)}) collective-permute-start(bf16[1,8,2176]{2,1,0:T(8,128)(2,1)} %bitcast.3), channel_id=1, source_target_pairs={{0,24},{2,26},{4,28},{6,30},{8,16},{10,18},{12,20},{14,22},{16,8},... | collective-permute-start | bytes 104456 | tf_op jit(solution)/shard_map/ppermute | solution.py:235
  7.4 5.0 %collective-permute-start.1 = (bf16[1,8,2176]{2,1,0:T(8,128)(2,1)}, bf16[1,8,2176]{2,1,0:T(8,128)(2,1)S(1)}, u32[]{:S(2)}, u32[]{:S(2)}) collective-permute-start(bf16[1,8,2176]{2,1,0:T(8,128)(2,1)} %bitcast.4), channel_id=1, source_target_pairs={{0,16},{2,18},{4,20},{6,22},{8,24},{10,26},{12,28},{14,30},{16,0},... | collective-permute-start | bytes 104456 | tf_op jit(solution)/shard_map/ppermute | solution.py:235
  7.4 5.0 %collective-permute-start = (bf16[1,8,2176]{2,1,0:T(8,128)(2,1)}, bf16[1,8,2176]{2,1,0:T(8,128)(2,1)S(1)}, u32[]{:S(2)}, u32[]{:S(2)}) collective-permute-start(bf16[1,8,2176]{2,1,0:T(8,128)(2,1)} %bitcast.5), channel_id=1, source_target_pairs={{0,8},{2,10},{4,12},{6,14},{8,0},{10,2},{12,4},{14,6},{16,24},{18,... | collective-permute-start | bytes 104456 | tf_op jit(solution)/shard_map/ppermute | solution.py:235
  13.3 3.6 %copy-start = (bf16[4,8,2176]{2,1,0:T(8,128)(2,1)}, bf16[4,8,2176]{2,1,0:T(8,128)(2,1)S(1)}, u32[]{:S(2)}) copy-start(bf16[4,8,2176]{2,1,0:T(8,128)(2,1)S(1)} %pad_maximum_fusion.held_ref) | copy-start | bytes 417796
  13.3 7.5 %collective-permute-start.5 = (bf16[4,8,2176]{2,1,0:T(8,128)(2,1)S(1)}, bf16[4,8,2176]{2,1,0:T(8,128)(2,1)S(1)}, u32[]{:S(2)}, u32[]{:S(2)}) collective-permute-start(bf16[4,8,2176]{2,1,0:T(8,128)(2,1)S(1)} %pad_maximum_fusion.held_ref), channel_id=1, source_target_pairs={{0,6},{2,4},{4,2},{6,0},{8,14},{10,12},{12,10},{14,8},{16,22},{18,... | collective-permute-start | bytes 417800 | tf_op jit(solution)/shard_map/ppermute | solution.py:235
  15.8 5.8 %collective-permute-start.4 = (bf16[4,8,2176]{2,1,0:T(8,128)(2,1)S(1)}, bf16[4,8,2176]{2,1,0:T(8,128)(2,1)S(1)}, u32[]{:S(2)}, u32[]{:S(2)}) collective-permute-start(bf16[4,8,2176]{2,1,0:T(8,128)(2,1)S(1)} %pad_maximum_fusion.held_ref), channel_id=1, source_target_pairs={{0,4},{2,6},{4,0},{6,2},{8,12},{10,14},{12,8},{14,10},{16,20},{18,... | collective-permute-start | bytes 417800 | tf_op jit(solution)/shard_map/ppermute | solution.py:235
  16.3 5.3 %collective-permute-start.3 = (bf16[4,8,2176]{2,1,0:T(8,128)(2,1)S(1)}, bf16[4,8,2176]{2,1,0:T(8,128)(2,1)S(1)}, u32[]{:S(2)}, u32[]{:S(2)}) collective-permute-start(bf16[4,8,2176]{2,1,0:T(8,128)(2,1)S(1)} %pad_maximum_fusion.held_ref), channel_id=1, source_target_pairs={{0,2},{2,0},{4,6},{6,4},{8,10},{10,8},{12,14},{14,12},{16,18},{18,... | collective-permute-start | bytes 417800 | tf_op jit(solution)/shard_map/ppermute | solution.py:235
  20.8 0.8 %copy-start.1 = (bf16[4,8,2176]{2,1,0:T(8,128)(2,1)}, bf16[4,8,2176]{2,1,0:T(8,128)(2,1)S(1)}, u32[]{:S(2)}) copy-start(bf16[4,8,2176]{2,1,0:T(8,128)(2,1)S(1)} %collective-permute-done.5.refs_2_) | copy-start | bytes 417796
  21.6 0.7 %copy-start.2 = (bf16[4,8,2176]{2,1,0:T(8,128)(2,1)}, bf16[4,8,2176]{2,1,0:T(8,128)(2,1)S(1)}, u32[]{:S(2)}) copy-start(bf16[4,8,2176]{2,1,0:T(8,128)(2,1)S(1)} %collective-permute-done.4.refs_1_) | copy-start | bytes 417796
  21.6 0.7 %copy-start.3 = (bf16[4,8,2176]{2,1,0:T(8,128)(2,1)}, bf16[4,8,2176]{2,1,0:T(8,128)(2,1)S(1)}, u32[]{:S(2)}) copy-start(bf16[4,8,2176]{2,1,0:T(8,128)(2,1)S(1)} %collective-permute-done.3.refs_0_) | copy-start | bytes 417796
